TPU v7x, 128 devices: a whole 4x4x4 slice. The times are simulated.
128 devices in a mesh: band: 8 (over y, x_lo), chan: 16 (over x_hi, z, core).
Axes of the slice: x: 4 (x_hi: 2, x_lo: 2; x = x_hi * 2 + x_lo), y: 4, z: 4, core: 2. Of those that a mesh axis runs over, the one named last changes fastest.
Arguments:
- coeffs: bfloat16 [2, 8, 1024, 8192], P(None, None, 'chan', 'band'), may hold values from -1100 to 1100, as said below
Outputs:
- coherence: float32 [1024, 1024], P('chan', 'band')
Inputs may be any that keep to these rules, and one draw needn't show every extreme that they name: `coeffs`: finite real and imaginary parts.
All inputs are finite; a program needn't handle non-finite values.
Results may differ from a plain program's by a relative error of at most 0.0003.
Values may be sent and summed in bfloat16 or wider, within the bound.
A program may use at most 192 MiB of HBM per device.

v0:
```python
import jax
import jax.numpy as jnp
from jax import lax
from jax.sharding import PartitionSpec as P

K = 8
W = 16
epsilon = 1e-06


def in_blocks(shard, dim, length):
    dims = shard.shape
    tiles = shard.reshape(*dims[:dim], length, dims[dim] // length, *dims[dim + 1 :])
    return jnp.moveaxis(tiles, dim, 0)


def sent_and_summed(shard, axis, dim):
    length = lax.axis_size(axis)
    tiles = lax.all_to_all(in_blocks(shard, dim, length), axis, 0, 0, tiled=True)
    return jnp.sum(tiles, axis=0)


def body(coeffs):
    num_bands = coeffs.shape[3] // W
    own_width = coeffs.shape[2]
    cycle_size = lax.axis_size("chan")
    own_index = lax.axis_index("chan")
    full_width = own_width * cycle_size
    group_count = lax.axis_size("band")
    scale = jnp.float32(W * K / (num_bands * group_count))
    local_rows = coeffs.reshape(2, K, own_width, num_bands, W)
    paired = jnp.stack((local_rows[1], -local_rows[0]), axis=0)
    left_side = jnp.concatenate((local_rows, paired), axis=2)
    wide_rows = local_rows.astype(jnp.float32)
    own_power = jnp.sum(wide_rows * wide_rows, axis=(0, 1, 4)).T + epsilon
    piece = lax.all_gather(coeffs, "chan", axis=2, tiled=True)
    count = piece.shape[2]
    right_side = piece.reshape(2, K, count, num_bands, W)
    product = jnp.einsum(
        "pkinw,pkjnw->nij", left_side, right_side, preferred_element_type=jnp.float32
    )
    real_part = product[:, :own_width, :]
    imag_part = product[:, own_width:, :]
    wide_piece = right_side.astype(jnp.float32)
    piece_power = jnp.sum(wide_piece * wide_piece, axis=(0, 1, 4)).T + epsilon
    coh_band = (real_part * real_part + imag_part * imag_part) / (
        own_power[:, :, None] * piece_power[:, None, :]
    )
    partial_value = jnp.sum(coh_band, axis=0)
    row_global = lax.broadcasted_iota(jnp.int32, (own_width, full_width), 0) + own_index * own_width
    col_global = lax.broadcasted_iota(jnp.int32, (own_width, full_width), 1)
    partial_value = jnp.where(row_global == col_global, jnp.float32(0.0), partial_value)
    result = sent_and_summed(partial_value, "band", 1)
    return result * scale


def solution(mesh):
    return jax.shard_map(
        body,
        mesh=mesh,
        in_specs=(P(None, None, "chan", "band"),),
        out_specs=P("chan", "band"),
        check_vma=False,
    )
```

profile of v0, /device:TPU:0, one launch (start us, length us, event | category | flops | bytes accessed | tf_op | source)
XLA Modules:
  0.0 327.6 jit_solution(6133088543758207707)
XLA Ops:
  6.5 0.0 copy-start
  6.5 0.0 all-gather.2.cloned.1.call-start
  6.5 4.2 %copy.37 = bf16[2,8,64,1024]{3,1,0,2:T(8,128)(2,1)} copy(bf16[2,8,64,1024]{3,2,1,0:T(8,128)(2,1)} %param.1) | data formatting | bytes 4194304 | tf_op args[0]
  10.7 0.0 all-gather.2.cloned.1.call-update
  10.8 0.0 copy-done
  10.8 3.2 copy.31
  14.0 0.4 multiply_reduce_fusion.1
  14.4 0.2 copy.40
  14.6 0.1 bitcast_reduce_fusion.1
  14.7 4.0 %fusion.14 = (bf16[1,8,64,1024]{2,3,1,0:T(8,128)(2,1)S(1)}, bf16[1,8,64,1024]{2,3,1,0:T(8,128)(2,1)}) fusion(bf16[2,8,64,1024]{2,3,1,0:T(8,128)(2,1)} %copy.31), kind=kLoop, calls=%fused_computation.25 | loop fusion | flops 524288 | bytes 4194304 | tf_op jit(solution)/shard_map/slice | solution.py:32
  18.7 180.3 %all-gather.2.cloned.1.call-done = bf16[2,8,1024,1024]{3,1,0,2:T(8,128)(2,1)} async-done(((bf16[2,8,64,1024]{3,1,0,2:T(8,128)(2,1)}), bf16[2,8,1024,1024]{3,1,0,2:T(8,128)(2,1)}) %all-gather.2.cloned.1.call-update) | async-done | bytes 33554448 | tf_op jit(solution)/shard_map/all_gather | solution.py:36
  199.1 18.3 %multiply_reduce_fusion = f32[1024,1024]{1,0:T(8,128)} fusion(bf16[2,8,1024,1024]{3,1,0,2:T(8,128)(2,1)} %all-gather.2.cloned.1.call-done), kind=kLoop, calls=%fused_computation | loop fusion | flops 49283072 | bytes 37748736 | tf_op jit(solution)/shard_map/reduce_sum | solution.py:45
  217.3 5.3 %copy.41 = f32[1024,1024]{0,1:T(8,128)} copy(f32[1024,1024]{1,0:T(8,128)} %multiply_reduce_fusion) | data formatting | bytes 8388608 | tf_op jit(solution)/shard_map/reduce_sum | solution.py:45
  222.7 3.1 bitcast_reduce_fusion
  225.8 45.1 %copy.38 = bf16[2,8,1024,1024]{2,3,1,0:T(8,128)(2,1)} copy(bf16[2,8,1024,1024]{3,1,0,2:T(8,128)(2,1)} %all-gather.2.cloned.1.call-done) | data formatting | bytes 67108864 | tf_op jit(solution)/shard_map/all_gather | solution.py:36
  271.0 25.2 %fusion.5 = f32[64,128,1024]{2,1,0:T(8,128)} fusion(bf16[2,8,1024,64,16]{2,4,3,1,0:T(8,128)(2,1)} %bitcast.24, bf16[1,8,64,64,16]{2,4,0,3,1:T(8,128)(2,1)} %bitcast.27, bf16[1,8,64,64,16]{2,4,0,3,1:T(8,128)(2,1)S(1)} %bitcast.26, bf16[2,8,64,64,16]{2,4,3,1,0:T(8,128)(2,1)} %bitcast.25), kind=kOutput, calls=%fused_computation.8 | convolution fusion | flops 4307550208 | bytes 71303168 | tf_op jit(solution)/shard_map/pkinw,pkjnw->nij/dot_general | solution.py:39
  296.2 11.9 %fusion.4 = f32[64,1024]{1,0:T(8,128)S(1)} fusion(f32[64,128,1024]{2,1,0:T(8,128)} %fusion.5, f32[64,1024]{1,0:T(8,128)S(1)} %add_bitcast_fusion, f32[64,64]{1,0:T(8,128)S(1)} %add_bitcast_fusion.1), kind=kLoop, calls=%fused_computation.7 | loop fusion | flops 25100288 | bytes 34095104 | tf_op jit(solution)/shard_map/reduce_sum | solution.py:49
  308.1 0.1 bitcast_select_fusion
  308.3 0.1 copy.42
  308.3 11.8 %all_to_all.5 = f32[8,64,128]{2,1,0:T(8,128)S(1)} all-to-all(f32[8,64,128]{2,1,0:T(8,128)S(1)} %copy.42), channel_id=1, replica_groups=mesh['band'=8,'chan'=16] {'band'}, dimensions={0} | all-to-all | bytes 524288 | tf_op jit(solution)/shard_map/all_to_all | solution.py:19
  320.1 0.6 broadcast_multiply_fusion
  (6 shorter events, 0.1 us)
Async XLA Ops:
  6.5 4.2 %copy-start = (bf16[2,8,64,1024]{3,2,1,0:T(8,128)(2,1)S(1)}, bf16[2,8,64,1024]{3,2,1,0:T(8,128)(2,1)}, u32[]{:S(2)}) copy-start(bf16[2,8,64,1024]{3,2,1,0:T(8,128)(2,1)} %param.1) | copy-start | bytes 6291460
  6.5 192.5 %all-gather.2.cloned.1.call-start = ((), (), s32[]{:S(2)}) async-start(), calls=%async_computation.1 | async-start | bytes 35651584 | tf_op jit(solution)/shard_map/all_gather | solution.py:36
Sparse Core Ops, SparseCore 0:
  10.9 188.1 all-gather.1
where the time goes:
time: 329 us; the launch traced here: 328 us
  waiting for transfers between devices  180 us (55%)
  local copies, waits for them, and re-layouts  58.2 us (18%)
  other arithmetic  38.6 us (12%)
  matrix products  25.2 us (8%)
  between operations  13.5 us (4%)
  blocking collectives  11.8 us (4%)
    all_gather x1, waiting for transfers between devices, body(): piece = lax.all_gather(coeffs, 'chan', axis=2, tiled=True)  180 us
    all_gather x1, local copies, waits for them, and re-layouts, body(): piece = lax.all_gather(coeffs, 'chan', axis=2, tiled=True)  45.1 us
    dot_general x1, matrix products, body(): jnp.einsum('pkinw,pkjnw->nij', left_side, right_side, preferred_element_t...  25.2 us
    reduce_sum x2, other arithmetic, body(): piece_power = jnp.sum(wide_piece * wide_piece, axis=(0, 1, 4)).T + epsilon  21.4 us
    reduce_sum x1, other arithmetic, body(): partial_value = jnp.sum(coh_band, axis=0)  11.9 us
    all_to_all x1, blocking collectives, sent_and_summed(): lax.all_to_all(in_blocks(shard, dim, length), axis, 0, 0, tiled=True)  11.8 us
    unnamed x5, local copies, waits for them, and re-layouts  7.43 us
  transfers between devices with their start and end apart: 1, of which 1 were waited for; matrix products, arithmetic and copies ran while one was open for 2% of the time, Pallas kernels for 0%

commit v1 on v0

--- a/solution.py
+++ b/solution.py
@@ -2,10 +2,18 @@
 import jax.numpy as jnp
 from jax import lax
 from jax.sharding import PartitionSpec as P
+from jax.lax import all_to_all, psum
 
 K = 8
 W = 16
 epsilon = 1e-06
+
+
+def fix_steps_all(w_in):
+    y1 = jnp.stack(tuple((w_in for _ in range(psum(1, axis_name="chan")))))
+    finding = all_to_all(y1, concat_axis=0, axis_name="chan", split_axis=0)
+    outcome_arr = jnp.concatenate(finding, 2)
+    return outcome_arr
 
 
 def in_blocks(shard, dim, length):
@@ -33,7 +41,7 @@
     left_side = jnp.concatenate((local_rows, paired), axis=2)
     wide_rows = local_rows.astype(jnp.float32)
     own_power = jnp.sum(wide_rows * wide_rows, axis=(0, 1, 4)).T + epsilon
-    piece = lax.all_gather(coeffs, "chan", axis=2, tiled=True)
+    piece = fix_steps_all(coeffs)
     count = piece.shape[2]
     right_side = piece.reshape(2, K, count, num_bands, W)
     product = jnp.einsum(

time: 329 us -> 802 us (2.44); the launches traced: 328 us -> 792 us
  waiting for transfers between devices: 180 us -> 517 us
  local copies, waits for them, and re-layouts: 58.2 us -> 196 us
  between operations: 13.5 us -> 0.12 us
  starting transfers between devices: 0.01 us -> 8.19 us
    all_to_all x0 -> x1, waiting for transfers between devices: none -> 517 us  [fix_steps_all(): finding = all_to_all(y1, concat_axis=0, axis_name='chan', split_axis=0)]
    all_gather x1 -> x0, waiting for transfers between devices: 180 us -> none  [body(): piece = lax.all_gather(coeffs, 'chan', axis=2, tiled=True)]
    another operation x0 -> x2, local copies, waits for them, and re-layouts: none -> 99.1 us  [the longest x1 86.9 us: body(): right_side = piece.reshape(2, K, count, num_bands, W)]
    reshape x0 -> x1, local copies, waits for them, and re-layouts: none -> 77.6 us  [fix_steps_all(): outcome_arr = jnp.concatenate(finding, 2)]
    all_gather x1 -> x0, local copies, waits for them, and re-layouts: 45.1 us -> none  [body(): piece = lax.all_gather(coeffs, 'chan', axis=2, tiled=True)]
    reduce_sum x1 -> x2, local copies, waits for them, and re-layouts: 5.34 us -> 15.7 us  [body(): piece_power = jnp.sum(wide_piece * wide_piece, axis=(0, 1, 4)).T + epsilon]
    all_to_all x0 -> x1, starting transfers between devices: none -> 8.19 us  [fix_steps_all(): finding = all_to_all(y1, concat_axis=0, axis_name='chan', split_axis=0)]
  transfers between devices with their start and end apart: 1 -> 1, of which waited for: 1 -> 1; matrix products, arithmetic and copies ran while one was open for 2% -> 1% of each run, Pallas kernels for 0% -> 0%
where the time goes in v1:
time: 802 us; the launch traced here: 792 us
  waiting for transfers between devices  517 us (64%)
  local copies, waits for them, and re-layouts  196 us (24%)
  other arithmetic  33.8 us (4%)
  matrix products  25.2 us (3%)
  blocking collectives  11.6 us (1%)
  starting transfers between devices  8.19 us (1%)
    all_to_all x1, waiting for transfers between devices, fix_steps_all(): finding = all_to_all(y1, concat_axis=0, axis_name='chan', split_axis=0)  517 us
    another operation x1, local copies, waits for them, and re-layouts, body(): right_side = piece.reshape(2, K, count, num_bands, W)  86.9 us
    reshape x1, local copies, waits for them, and re-layouts, fix_steps_all(): outcome_arr = jnp.concatenate(finding, 2)  77.6 us
    dot_general x1, matrix products, body(): jnp.einsum('pkinw,pkjnw->nij', left_side, right_side, preferred_element_t...  25.2 us
    reduce_sum x2, other arithmetic, body(): piece_power = jnp.sum(wide_piece * wide_piece, axis=(0, 1, 4)).T + epsilon  16.6 us
  transfers between devices with their start and end apart: 1, of which 1 were waited for; matrix products, arithmetic and copies ran while one was open for 1% of the time, Pallas kernels for 0%

profile of v1, /device:TPU:0, one launch (start us, length us, event | category | flops | bytes accessed | tf_op | source)
XLA Modules:
  0.0 792.1 jit_solution(12360225404881714423)
XLA Ops:
  0.0 12.2 %stack.5 = bf16[16,2,8,64,1024]{4,3,2,1,0:T(8,128)(2,1)} broadcast(bf16[2,8,64,1024]{3,2,1,0:T(8,128)(2,1)} %param.1), dimensions={1,2,3,4} | broadcast | bytes 35651584 | tf_op jit(solution)/shard_map/stack | solution.py:13
  12.2 0.0 copy-start
  12.2 8.2 %all-to-all-start = ((bf16[16,2,8,64,1024]{4,3,2,1,0:T(8,128)(2,1)}), bf16[16,2,8,64,1024]{4,3,2,1,0:T(8,128)(2,1)}, u32[]{:S(2)}, u32[]{:S(2)}) async-start(bf16[16,2,8,64,1024]{4,3,2,1,0:T(8,128)(2,1)} %stack.5), calls=%async_computation | async-start | bytes 67108864 | tf_op jit(solution)/shard_map/all_to_all | solution.py:14
  20.4 0.0 copy-done
  20.4 3.1 copy.29
  23.5 0.4 multiply_reduce_fusion.1
  23.9 0.2 copy.37
  24.2 0.1 bitcast_reduce_fusion
  24.3 3.9 fusion.14
  28.2 517.5 %all-to-all-done = bf16[16,2,8,64,1024]{4,3,2,1,0:T(8,128)(2,1)} async-done(((bf16[16,2,8,64,1024]{4,3,2,1,0:T(8,128)(2,1)}), bf16[16,2,8,64,1024]{4,3,2,1,0:T(8,128)(2,1)}, u32[]{:S(2)}, u32[]{:S(2)}) %all-to-all-start) | async-done | bytes 33554464 | tf_op jit(solution)/shard_map/all_to_all | solution.py:14
  545.7 13.5 %multiply_reduce_fusion = f32[16,64,1024]{2,1,0:T(8,128)} fusion(bf16[16,2,8,64,1024]{4,3,2,1,0:T(8,128)(2,1)} %all-to-all-done), kind=kLoop, calls=%fused_computation | loop fusion | flops 49283072 | bytes 37748736 | tf_op jit(solution)/shard_map/reduce_sum | solution.py:53
  559.3 8.1 %copy.38 = f32[16,64,1024]{1,0,2:T(8,128)} copy(f32[16,64,1024]{2,1,0:T(8,128)} %multiply_reduce_fusion) | data formatting | bytes 8388608 | tf_op jit(solution)/shard_map/reduce_sum | solution.py:53
  567.3 7.6 reduce_sum.56
  575.0 3.1 reduce_sum.57
  578.1 77.6 %copy.35 = bf16[2,8,16,64,1024]{3,2,4,1,0:T(8,128)(2,1)} copy(bf16[2,8,16,64,1024]{4,3,1,0,2:T(8,128)(2,1)} %bitcast.5) | data formatting | bytes 67108864 | tf_op jit(solution)/shard_map/reshape | solution.py:15
  655.7 86.9 %reshape_reshape.3 = bf16[2,8,1024,64,16]{2,4,3,1,0:T(8,128)(2,1)} reshape(bf16[2,8,16,64,1024]{3,2,4,1,0:T(8,128)(2,1)} %copy.35) | data formatting | bytes 67108864 | tf_op jit(solution)/shard_map/reshape;reshape | solution.py:46
  742.6 25.2 %fusion.5 = f32[64,128,1024]{2,1,0:T(8,128)} fusion(bf16[2,8,1024,64,16]{2,4,3,1,0:T(8,128)(2,1)} %reshape_reshape.3, bf16[1,8,64,64,16]{2,4,0,3,1:T(8,128)(2,1)} %bitcast.31, bf16[1,8,64,64,16]{2,4,0,3,1:T(8,128)(2,1)S(1)} %bitcast.30, bf16[2,8,64,64,16]{2,4,3,1,0:T(8,128)(2,1)} %bitcast.29), kind=kOutput, calls=%fused_computation.8 | convolution fusion | flops 4307550208 | bytes 71303168 | tf_op jit(solution)/shard_map/pkinw,pkjnw->nij/dot_general | solution.py:47
  767.8 11.9 %fusion.4 = f32[64,1024]{1,0:T(8,128)S(1)} fusion(f32[64,128,1024]{2,1,0:T(8,128)} %fusion.5, f32[64,1024]{1,0:T(8,128)S(1)} %add_bitcast_fusion, f32[64,64]{1,0:T(8,128)S(1)} %add_bitcast_fusion.1), kind=kLoop, calls=%fused_computation.7 | loop fusion | flops 25100288 | bytes 34095104 | tf_op jit(solution)/shard_map/reduce_sum | solution.py:57
  779.7 0.1 bitcast_select_fusion
  779.9 0.1 copy.39
  779.9 11.6 %all_to_all.10 = f32[8,64,128]{2,1,0:T(8,128)S(1)} all-to-all(f32[8,64,128]{2,1,0:T(8,128)S(1)} %copy.39), channel_id=1, replica_groups=mesh['band'=8,'chan'=16] {'band'}, dimensions={0} | all-to-all | bytes 524288 | tf_op jit(solution)/shard_map/all_to_all | solution.py:27
  791.5 0.6 broadcast_multiply_fusion
  (6 shorter events, 0.1 us)
Async XLA Ops:
  12.2 8.2 %copy-start = (bf16[2,8,64,1024]{3,2,1,0:T(8,128)(2,1)S(1)}, bf16[2,8,64,1024]{3,2,1,0:T(8,128)(2,1)}, u32[]{:S(2)}) copy-start(bf16[2,8,64,1024]{3,2,1,0:T(8,128)(2,1)} %param.1) | copy-start | bytes 6291460
  12.2 533.5 %all-to-all-start = ((bf16[16,2,8,64,1024]{4,3,2,1,0:T(8,128)(2,1)}), bf16[16,2,8,64,1024]{4,3,2,1,0:T(8,128)(2,1)}, u32[]{:S(2)}, u32[]{:S(2)}) async-start(bf16[16,2,8,64,1024]{4,3,2,1,0:T(8,128)(2,1)} %stack.5), calls=%async_computation | async-start | bytes 67108864 | tf_op jit(solution)/shard_map/all_to_all | solution.py:14
